TPU v7x, 32 devices: a whole 2x2x4 slice. The times are simulated.
32 devices in a mesh: band: 8 (over z, x), space: 4 (over y, core).
Axes of the slice: x: 2, y: 2, z: 4, core: 2. Of those that a mesh axis runs over, the one named last changes fastest.
Arguments:
- orbitals: bfloat16 [64, 64, 160, 128], P('band', None, 'space'), may hold values from -8.5 to 8.5
- occupations: float32 [64], P('band'), may hold values from 0.07 to 2.5
Outputs:
- potential: float32 [64, 160, 128], P('band', 'space')
All inputs are finite; a program needn't handle non-finite values.
Results may differ from a plain program's by a relative error of at most 0.0003.
Values sent between devices are 32-bit elements; how exact they have to be, the bound alone decides.
A program may use at most 64 MiB of HBM per device.

v0:
```python
import math
import jax
import jax.numpy as jnp
from jax import lax
from jax.sharding import PartitionSpec as P

ITERS = 3
four_pi = 4.0 * math.pi


def with_halo(shard, sides, width):
    for axis, dim in sides:
        peers, length = (lax.axis_size(axis), shard.shape[dim])
        up = [(i, (i + 1) % peers) for i in range(peers - 1)]
        down = [(j, i) for i, j in up]
        last = lax.slice_in_dim(shard, length - width, length, axis=dim)
        first = lax.slice_in_dim(shard, 0, width, axis=dim)
        before = lax.ppermute(last, axis, up)
        after = lax.ppermute(first, axis, down)
        shard = jnp.concatenate([before, shard, after], axis=dim)
    return shard


def stencil(padded):
    center = padded[2:-2, 2:-2, 2:-2]
    near = padded[3:-1, 2:-2, 2:-2] + padded[1:-3, 2:-2, 2:-2]
    near = near + padded[2:-2, 3:-1, 2:-2] + padded[2:-2, 1:-3, 2:-2]
    near = near + padded[2:-2, 2:-2, 3:-1] + padded[2:-2, 2:-2, 1:-3]
    distant = padded[4:, 2:-2, 2:-2] + padded[:-4, 2:-2, 2:-2]
    distant = distant + padded[2:-2, 4:, 2:-2] + padded[2:-2, :-4, 2:-2]
    distant = distant + padded[2:-2, 2:-2, 4:] + padded[2:-2, 2:-2, :-4]
    return 7.5 * center - 4.0 / 3.0 * near + 1.0 / 12.0 * distant


def operate(field):
    widened = with_halo(field, (("band", 0), ("space", 1)), 2)
    return stencil(jnp.pad(widened, ((0, 0), (0, 0), (2, 2))))


def paired_sums(residual, image):
    return lax.psum((jnp.sum(residual * residual), jnp.sum(residual * image)), ("band", "space"))


def local(orbitals, occupations):

    def accumulate(index, total):
        wave = lax.dynamic_index_in_dim(orbitals, index, 0, keepdims=False).astype(jnp.float32)
        return total + occupations[index] * wave * wave

    start = jnp.zeros(orbitals.shape[1:], jnp.float32)
    partial_value = lax.fori_loop(0, orbitals.shape[0], accumulate, start)
    groups = lax.axis_size("band")
    summed = lax.psum(partial_value, "band")
    share = orbitals.shape[1] // groups
    mine = lax.dynamic_slice_in_dim(summed, lax.axis_index("band") * share, share, 0)
    density = mine / (orbitals.shape[0] * groups)
    source = four_pi * density
    potential = jnp.zeros_like(source)
    residual = source
    image = operate(residual)
    norm_now, product = paired_sums(residual, image)
    alpha = norm_now / product
    direction, along = (residual, image)
    for step in range(ITERS):
        potential = potential + alpha * direction
        residual = residual - alpha * along
        if step + 1 < ITERS:
            image = operate(residual)
            norm_next, product = paired_sums(residual, image)
            ratio = norm_next / norm_now
            alpha = norm_next / (product - ratio * norm_next / alpha)
            direction = residual + ratio * direction
            along = image + ratio * along
            norm_now = norm_next
    return potential


def solution(mesh):
    in_specs = (P("band", None, "space", None), P("band"))
    out_specs = P("band", "space", None)
    return jax.shard_map(local, mesh=mesh, in_specs=in_specs, out_specs=out_specs, check_vma=False)
```

profile of v0, /device:TPU:0, one launch (start us, length us, event | category | flops | bytes accessed | tf_op | source)
XLA Modules:
  0.0 320.6 jit_solution(14691085561565989361)
XLA Ops:
  6.5 0.0 all-reduce.8.cloned.1.call-start
  6.5 30.2 %while.14 = (s32[]{:T(128)}, f32[64,40,128]{2,1,0:T(8,128)S(1)}, f32[8]{0:T(128)}, bf16[8,64,40,128]{3,2,1,0:T(8,128)(2,1)}, s32[]{:T(128)}, /*index=5*/s32[]{:T(128)}) while((s32[]{:T(128)}, f32[64,40,128]{2,1,0:T(8,128)S(1)}, f32[8]{0:T(128)}, bf16[8,64,40,128]{3,2,1,0:T(8,128)(2,1)}, s32[]{:T(128)}, /*index=5*/s32[]{:T(128)}) %tuple.46), condition=%wide.region_1.2_spmd.clone, body=%wide.region_0.1_spmd.clone.sunk | while | flops 1638403 | bytes 3276907 | solution.py:51
  6.5 1.3 dynamic_slice.31
  7.8 2.5 fusion.46
  10.3 1.3 dynamic_slice.31
  11.6 2.5 fusion.46
  14.1 1.3 dynamic_slice.31
  15.4 2.5 fusion.46
  17.9 1.3 dynamic_slice.31
  19.2 2.5 fusion.46
  21.6 1.3 dynamic_slice.31
  22.9 2.5 fusion.46
  25.4 1.3 dynamic_slice.31
  26.7 2.5 fusion.46
  29.2 1.3 dynamic_slice.31
  30.5 2.5 fusion.46
  33.0 1.3 dynamic_slice.31
  34.3 2.5 fusion.46
  36.7 0.0 copy-start
  36.8 1.1 copy-done
  37.8 0.0 all-reduce.8.cloned.1.call-update
  37.9 86.5 %all-reduce.8.cloned.1.call-done = f32[64,40,128]{2,1,0:T(8,128)} async-done(((f32[64,40,128]{2,1,0:T(8,128)}), f32[64,40,128]{2,1,0:T(8,128)}) %all-reduce.8.cloned.1.call-update) | async-done | bytes 1310736 | tf_op jit(solution)/shard_map/psum | solution.py:53
  124.4 0.9 dynamic-slice_multiply_fusion
  125.3 3.4 %collective-permute-start.1 = (f32[2,40,128]{2,1,0:T(8,128)S(1)}, f32[2,40,128]{2,1,0:T(8,128)S(1)}, u32[]{:S(2)}, u32[]{:S(2)}) collective-permute-start(f32[2,40,128]{2,1,0:T(8,128)S(1)} %get-tuple-element.138), channel_id=1, source_target_pairs={{0,4},{4,8},{8,12},{12,16},{16,20},{20,24},{24,28},{1,5},{5,9},{9,... | collective-permute-start | bytes 122888 | tf_op jit(solution)/shard_map/ppermute | solution.py:18
  128.7 1.3 collective-permute-start
  130.0 0.4 collective-permute-done.1
  130.3 4.2 %collective-permute-done = f32[2,40,128]{2,1,0:T(8,128)S(1)} collective-permute-done((f32[2,40,128]{2,1,0:T(8,128)S(1)}, f32[2,40,128]{2,1,0:T(8,128)S(1)}, u32[]{:S(2)}, u32[]{:S(2)}) %collective-permute-start) | collective-permute-done | bytes 40992 | tf_op jit(solution)/shard_map/ppermute | solution.py:19
  134.6 1.3 collective-permute-start.3
  135.9 1.3 collective-permute-start.2
  137.2 0.0 collective-permute-done.3
  137.2 3.5 %collective-permute-done.2 = f32[12,2,128]{2,1,0:T(2,128)S(1)} collective-permute-done((f32[12,2,128]{2,1,0:T(2,128)S(1)}, f32[12,2,128]{2,1,0:T(2,128)S(1)}, u32[]{:S(2)}, u32[]{:S(2)}) %collective-permute-start.2) | collective-permute-done | bytes 12320 | tf_op jit(solution)/shard_map/ppermute | solution.py:19
  140.7 0.3 select_maximum_fusion.8
  141.0 1.8 multiply_reduce_fusion.3
  142.8 41.2 %all-reduce.5 = (f32[]{:T(128)}, f32[]{:T(128)}) all-reduce(f32[]{:T(128)} %get-tuple-element.105, f32[]{:T(128)} %get-tuple-element.104), channel_id=1, replica_groups=mesh['band'=8,'space'=4] {'band','space'}, use_global_device_ids=true, to_apply=%region_4.5 | all-reduce | flops 2 | bytes 16 | tf_op jit(solution)/shard_map/psum | solution.py:41
  185.3 0.9 multiply_subtract_fusion.1
  186.3 4.2 %collective-permute-start.5 = (f32[2,40,128]{2,1,0:T(8,128)S(1)}, f32[2,40,128]{2,1,0:T(8,128)S(1)}, u32[]{:S(2)}, u32[]{:S(2)}) collective-permute-start(f32[2,40,128]{2,1,0:T(8,128)S(1)} %get-tuple-element.136), channel_id=1, source_target_pairs={{0,4},{4,8},{8,12},{12,16},{16,20},{20,24},{24,28},{1,5},{5,9},{9,... | collective-permute-start | bytes 122888 | tf_op jit(solution)/shard_map/ppermute | solution.py:18
  190.5 1.3 collective-permute-start.4
  191.8 0.4 collective-permute-done.5
  192.1 4.2 %collective-permute-done.4 = f32[2,40,128]{2,1,0:T(8,128)S(1)} collective-permute-done((f32[2,40,128]{2,1,0:T(8,128)S(1)}, f32[2,40,128]{2,1,0:T(8,128)S(1)}, u32[]{:S(2)}, u32[]{:S(2)}) %collective-permute-start.4) | collective-permute-done | bytes 40992 | tf_op jit(solution)/shard_map/ppermute | solution.py:19
  196.4 1.3 collective-permute-start.7
  197.7 1.3 collective-permute-start.6
  199.0 0.0 collective-permute-done.7
  199.0 2.8 collective-permute-done.6
  201.8 0.3 select_maximum_fusion.4
  202.1 0.9 multiply_reduce_fusion.1
  203.0 41.9 %all-reduce.4 = (f32[]{:T(128)}, f32[]{:T(128)}) all-reduce(f32[]{:T(128)} %get-tuple-element.103, f32[]{:T(128)} %get-tuple-element.102), channel_id=1, replica_groups=mesh['band'=8,'space'=4] {'band','space'}, use_global_device_ids=true, to_apply=%region_8.9 | all-reduce | flops 2 | bytes 16 | tf_op jit(solution)/shard_map/psum | solution.py:41
  249.4 4.2 %collective-permute-start.9 = (f32[2,40,128]{2,1,0:T(8,128)S(1)}, f32[2,40,128]{2,1,0:T(8,128)S(1)}, u32[]{:S(2)}, u32[]{:S(2)}) collective-permute-start(f32[2,40,128]{2,1,0:T(8,128)S(1)} %get-tuple-element.134), channel_id=1, source_target_pairs={{0,4},{4,8},{8,12},{12,16},{16,20},{20,24},{24,28},{1,5},{5,9},{9,... | collective-permute-start | bytes 122888 | tf_op jit(solution)/shard_map/ppermute | solution.py:18
  253.6 1.3 collective-permute-start.8
  254.9 0.4 collective-permute-done.9
  255.2 4.2 %collective-permute-done.8 = f32[2,40,128]{2,1,0:T(8,128)S(1)} collective-permute-done((f32[2,40,128]{2,1,0:T(8,128)S(1)}, f32[2,40,128]{2,1,0:T(8,128)S(1)}, u32[]{:S(2)}, u32[]{:S(2)}) %collective-permute-start.8) | collective-permute-done | bytes 40992 | tf_op jit(solution)/shard_map/ppermute | solution.py:19
  259.5 1.3 collective-permute-start.11
  260.8 1.3 collective-permute-start.10
  262.1 0.0 collective-permute-done.11
  262.1 3.1 collective-permute-done.10
  265.2 0.3 select_maximum_fusion
  265.6 0.9 fusion.39
  266.5 41.9 %all-reduce.3 = (f32[]{:T(128)}, f32[]{:T(128)}) all-reduce(f32[]{:T(128)} %get-tuple-element.101, f32[]{:T(128)} %get-tuple-element.100), channel_id=1, replica_groups=mesh['band'=8,'space'=4] {'band','space'}, use_global_device_ids=true, to_apply=%region_12.13 | all-reduce | flops 2 | bytes 16 | tf_op jit(solution)/shard_map/psum | solution.py:41
  312.1 1.6 multiply_add_fusion
  (11 shorter events, 0.2 us)
Async XLA Ops:
  6.5 117.8 %all-reduce.8.cloned.1.call-start = ((), (), s32[]{:S(2)}) async-start(), calls=%async_computation | async-start | bytes 2621440 | tf_op jit(solution)/shard_map/psum | solution.py:53
  36.7 1.1 copy-start
  125.3 5.0 %collective-permute-start.1 = (f32[2,40,128]{2,1,0:T(8,128)S(1)}, f32[2,40,128]{2,1,0:T(8,128)S(1)}, u32[]{:S(2)}, u32[]{:S(2)}) collective-permute-start(f32[2,40,128]{2,1,0:T(8,128)S(1)} %get-tuple-element.138), channel_id=1, source_target_pairs={{0,4},{4,8},{8,12},{12,16},{16,20},{20,24},{24,28},{1,5},{5,9},{9,... | collective-permute-start | bytes 122888 | tf_op jit(solution)/shard_map/ppermute | solution.py:18
  128.7 5.9 %collective-permute-start = (f32[2,40,128]{2,1,0:T(8,128)S(1)}, f32[2,40,128]{2,1,0:T(8,128)S(1)}, u32[]{:S(2)}, u32[]{:S(2)}) collective-permute-start(f32[2,40,128]{2,1,0:T(8,128)S(1)} %get-tuple-element.139), channel_id=1, source_target_pairs={{4,0},{8,4},{12,8},{16,12},{20,16},{24,20},{28,24},{5,1},{9,5},{13... | collective-permute-start | bytes 122888 | tf_op jit(solution)/shard_map/ppermute | solution.py:19
  134.6 2.6 collective-permute-start.3
  135.9 4.8 %collective-permute-start.2 = (f32[12,2,128]{2,1,0:T(2,128)S(1)}, f32[12,2,128]{2,1,0:T(2,128)S(1)}, u32[]{:S(2)}, u32[]{:S(2)}) collective-permute-start(f32[12,2,128]{2,1,0:T(2,128)S(1)} %get-tuple-element.133), channel_id=1, source_target_pairs={{1,0},{2,1},{3,2},{5,4},{6,5},{7,6},{9,8},{10,9},{11,10},{13,12},{... | collective-permute-start | bytes 36872 | tf_op jit(solution)/shard_map/ppermute | solution.py:19
  186.3 5.8 %collective-permute-start.5 = (f32[2,40,128]{2,1,0:T(8,128)S(1)}, f32[2,40,128]{2,1,0:T(8,128)S(1)}, u32[]{:S(2)}, u32[]{:S(2)}) collective-permute-start(f32[2,40,128]{2,1,0:T(8,128)S(1)} %get-tuple-element.136), channel_id=1, source_target_pairs={{0,4},{4,8},{8,12},{12,16},{16,20},{20,24},{24,28},{1,5},{5,9},{9,... | collective-permute-start | bytes 122888 | tf_op jit(solution)/shard_map/ppermute | solution.py:18
  190.5 5.9 %collective-permute-start.4 = (f32[2,40,128]{2,1,0:T(8,128)S(1)}, f32[2,40,128]{2,1,0:T(8,128)S(1)}, u32[]{:S(2)}, u32[]{:S(2)}) collective-permute-start(f32[2,40,128]{2,1,0:T(8,128)S(1)} %get-tuple-element.137), channel_id=1, source_target_pairs={{4,0},{8,4},{12,8},{16,12},{20,16},{24,20},{28,24},{5,1},{9,5},{13... | collective-permute-start | bytes 122888 | tf_op jit(solution)/shard_map/ppermute | solution.py:19
  196.4 2.6 collective-permute-start.7
  197.7 4.1 %collective-permute-start.6 = (f32[12,2,128]{2,1,0:T(2,128)S(1)}, f32[12,2,128]{2,1,0:T(2,128)S(1)}, u32[]{:S(2)}, u32[]{:S(2)}) collective-permute-start(f32[12,2,128]{2,1,0:T(2,128)S(1)} %get-tuple-element.129), channel_id=1, source_target_pairs={{1,0},{2,1},{3,2},{5,4},{6,5},{7,6},{9,8},{10,9},{11,10},{13,12},{... | collective-permute-start | bytes 36872 | tf_op jit(solution)/shard_map/ppermute | solution.py:19
  249.4 5.8 %collective-permute-start.9 = (f32[2,40,128]{2,1,0:T(8,128)S(1)}, f32[2,40,128]{2,1,0:T(8,128)S(1)}, u32[]{:S(2)}, u32[]{:S(2)}) collective-permute-start(f32[2,40,128]{2,1,0:T(8,128)S(1)} %get-tuple-element.134), channel_id=1, source_target_pairs={{0,4},{4,8},{8,12},{12,16},{16,20},{20,24},{24,28},{1,5},{5,9},{9,... | collective-permute-start | bytes 122888 | tf_op jit(solution)/shard_map/ppermute | solution.py:18
  253.6 5.9 %collective-permute-start.8 = (f32[2,40,128]{2,1,0:T(8,128)S(1)}, f32[2,40,128]{2,1,0:T(8,128)S(1)}, u32[]{:S(2)}, u32[]{:S(2)}) collective-permute-start(f32[2,40,128]{2,1,0:T(8,128)S(1)} %get-tuple-element.135), channel_id=1, source_target_pairs={{4,0},{8,4},{12,8},{16,12},{20,16},{24,20},{28,24},{5,1},{9,5},{13... | collective-permute-start | bytes 122888 | tf_op jit(solution)/shard_map/ppermute | solution.py:19
  259.5 2.6 collective-permute-start.11
  260.8 4.4 %collective-permute-start.10 = (f32[12,2,128]{2,1,0:T(2,128)S(1)}, f32[12,2,128]{2,1,0:T(2,128)S(1)}, u32[]{:S(2)}, u32[]{:S(2)}) collective-permute-start(f32[12,2,128]{2,1,0:T(2,128)S(1)} %get-tuple-element.125), channel_id=1, source_target_pairs={{1,0},{2,1},{3,2},{5,4},{6,5},{7,6},{9,8},{10,9},{11,10},{13,12},{... | collective-permute-start | bytes 36872 | tf_op jit(solution)/shard_map/ppermute | solution.py:19
Sparse Core Ops, SparseCore 0:
  38.0 86.3 all-reduce.7
where the time goes:
time: 322 us; the launch traced here: 321 us
  blocking collectives  125 us (39%)
  waiting for transfers between devices  110 us (34%)
  other arithmetic  27.8 us (9%)
  starting transfers between devices  23.4 us (7%)
  between operations  23 us (7%)
  local copies, waits for them, and re-layouts  11.5 us (4%)
    psum x3, blocking collectives, paired_sums(): lax.psum((jnp.sum(residual * residual), jnp.sum(residual * image)), ('ban...  125 us
    psum x1, waiting for transfers between devices, local(): summed = lax.psum(partial_value, 'band')  86.5 us
    ppermute x6, waiting for transfers between devices, with_halo(): after = lax.ppermute(first, axis, down)  22.1 us
    add x8, other arithmetic, accumulate(): return total + occupations[index] * wave * wave  19.6 us
    ppermute x6, starting transfers between devices, with_halo(): before = lax.ppermute(last, axis, up)  15.6 us
    dynamic_slice x8, local copies, waits for them, and re-layouts, accumulate(): return total + occupations[index] * wave * wave  10.4 us
    ppermute x6, starting transfers between devices, with_halo(): after = lax.ppermute(first, axis, down)  7.75 us
  transfers between devices with their start and end apart: 13, of which 10 were waited for; matrix products, arithmetic and copies ran while one was open for 0% of the time, Pallas kernels for 0%

commit v1 on v0

--- a/solution.py
+++ b/solution.py
@@ -50,7 +50,9 @@
     start = jnp.zeros(orbitals.shape[1:], jnp.float32)
     partial_value = lax.fori_loop(0, orbitals.shape[0], accumulate, start)
     groups = lax.axis_size("band")
-    summed = lax.psum(partial_value, "band")
+    summed = partial_value
+    for hop in (1, 2, 4):
+        summed = summed + lax.ppermute(summed, "band", [(dev, dev ^ hop) for dev in range(8)])
     share = orbitals.shape[1] // groups
     mine = lax.dynamic_slice_in_dim(summed, lax.axis_index("band") * share, share, 0)
     density = mine / (orbitals.shape[0] * groups)

time: 322 us -> 336 us (1.043)
  starting transfers between devices: 23.4 us -> 36.8 us
  between operations: 23 us -> 9.76 us
  waiting for transfers between devices: 110 us -> 123 us
  blocking collectives: 125 us -> 131 us
  other arithmetic: 27.8 us -> 23.8 us
    ppermute x0 -> x3, waiting for transfers between devices: none -> 112 us  [local(): lax.ppermute(summed, 'band', [(dev, dev ^ hop) for dev in range(8)])]
    psum x1 -> x0, waiting for transfers between devices: 86.5 us -> none  [local(): summed = lax.psum(partial_value, 'band')]
    ppermute x6, waiting for transfers between devices: 22.1 us -> 4.32 us  [with_halo(): after = lax.ppermute(first, axis, down)]
    ppermute x0 -> x3, starting transfers between devices: none -> 7.55 us  [local(): lax.ppermute(summed, 'band', [(dev, dev ^ hop) for dev in range(8)])]
    ppermute x6, starting transfers between devices: 15.6 us -> 21.5 us  [with_halo(): before = lax.ppermute(last, axis, up)]
    psum x3, blocking collectives: 125 us -> 131 us  [paired_sums(): lax.psum((jnp.sum(residual * residual), jnp.sum(residual * image)), ('ban...]
    ppermute x6, waiting for transfers between devices: 1.07 us -> 6.46 us  [with_halo(): before = lax.ppermute(last, axis, up)]
  transfers between devices with their start and end apart: 13 -> 15, of which waited for: 10 -> 9; matrix products, arithmetic and copies ran while one was open for 0% -> 0% of each run, Pallas kernels for 0% -> 0%
where the time goes in v1:
time: 336 us; the launch traced here: 334 us
  blocking collectives  131 us (39%)
  waiting for transfers between devices  123 us (37%)
  starting transfers between devices  36.8 us (11%)
  other arithmetic  23.8 us (7%)
  local copies, waits for them, and re-layouts  9.9 us (3%)
  between operations  9.76 us (3%)
    psum x3, blocking collectives, paired_sums(): lax.psum((jnp.sum(residual * residual), jnp.sum(residual * image)), ('ban...  131 us
    ppermute x3, waiting for transfers between devices, local(): lax.ppermute(summed, 'band', [(dev, dev ^ hop) for dev in range(8)])  112 us
    ppermute x6, starting transfers between devices, with_halo(): before = lax.ppermute(last, axis, up)  21.5 us
    add x8, other arithmetic, accumulate(): return total + occupations[index] * wave * wave  19 us
    dynamic_slice x8, local copies, waits for them, and re-layouts, accumulate(): return total + occupations[index] * wave * wave  9.87 us
    ppermute x6, starting transfers between devices, with_halo(): after = lax.ppermute(first, axis, down)  7.75 us
    ppermute x3, starting transfers between devices, local(): lax.ppermute(summed, 'band', [(dev, dev ^ hop) for dev in range(8)])  7.55 us
  transfers between devices with their start and end apart: 15, of which 9 were waited for; matrix products, arithmetic and copies ran while one was open for 0% of the time, Pallas kernels for 0%

profile of v1, /device:TPU:0, one launch (start us, length us, event | category | flops | bytes accessed | tf_op | source)
XLA Modules:
  0.0 334.3 jit_solution(8773211969972731633)
XLA Ops:
  0.0 29.0 %while.14 = (s32[]{:T(128)}, f32[64,40,128]{2,1,0:T(8,128)S(1)}, f32[8]{0:T(128)}, bf16[8,64,40,128]{3,2,1,0:T(8,128)(2,1)}, s32[]{:T(128)}, /*index=5*/s32[]{:T(128)}) while((s32[]{:T(128)}, f32[64,40,128]{2,1,0:T(8,128)S(1)}, f32[8]{0:T(128)}, bf16[8,64,40,128]{3,2,1,0:T(8,128)(2,1)}, s32[]{:T(128)}, /*index=5*/s32[]{:T(128)}) %tuple.47), condition=%wide.region_1.2_spmd.clone, body=%wide.region_0.1_spmd.clone.sunk | while | flops 1638403 | bytes 3276899 | solution.py:51
  0.0 1.2 dynamic_slice.31
  1.2 2.4 fusion.46
  3.6 1.2 dynamic_slice.31
  4.9 2.4 fusion.46
  7.3 1.2 dynamic_slice.31
  8.5 2.4 fusion.46
  10.9 1.2 dynamic_slice.31
  12.1 2.4 fusion.46
  14.5 1.2 dynamic_slice.31
  15.8 2.4 fusion.46
  18.2 1.2 dynamic_slice.31
  19.4 2.4 fusion.46
  21.8 1.2 dynamic_slice.31
  23.0 2.4 fusion.46
  25.4 1.2 dynamic_slice.31
  26.7 2.4 fusion.46
  29.0 3.0 collective-permute-start
  32.1 28.8 %collective-permute-done = f32[64,40,128]{2,1,0:T(8,128)S(1)} collective-permute-done((f32[64,40,128]{2,1,0:T(8,128)S(1)}, f32[64,40,128]{2,1,0:T(8,128)S(1)}, u32[]{:S(2)}, u32[]{:S(2)}) %collective-permute-start) | collective-permute-done | bytes 1310752 | tf_op jit(solution)/shard_map/ppermute | solution.py:55
  60.9 0.1 add.174
  61.0 1.9 collective-permute-start.1
  62.9 28.1 %collective-permute-done.1 = f32[64,40,128]{2,1,0:T(8,128)S(1)} collective-permute-done((f32[64,40,128]{2,1,0:T(8,128)S(1)}, f32[64,40,128]{2,1,0:T(8,128)S(1)}, u32[]{:S(2)}, u32[]{:S(2)}) %collective-permute-start.1) | collective-permute-done | bytes 1310752 | tf_op jit(solution)/shard_map/ppermute | solution.py:55
  91.0 0.1 add.175
  91.1 2.6 collective-permute-start.2
  93.8 55.5 %collective-permute-done.2 = f32[64,40,128]{2,1,0:T(8,128)S(1)} collective-permute-done((f32[64,40,128]{2,1,0:T(8,128)S(1)}, f32[64,40,128]{2,1,0:T(8,128)S(1)}, u32[]{:S(2)}, u32[]{:S(2)}) %collective-permute-start.2) | collective-permute-done | bytes 1310752 | tf_op jit(solution)/shard_map/ppermute | solution.py:55
  149.3 1.3 collective-permute-start.3
  150.6 4.5 %collective-permute-start.4 = (f32[2,40,128]{2,1,0:T(8,128)S(1)}, f32[2,40,128]{2,1,0:T(8,128)S(1)}, u32[]{:S(2)}, u32[]{:S(2)}) collective-permute-start(f32[2,40,128]{2,1,0:T(8,128)S(1)} %get-tuple-element.140), channel_id=1, source_target_pairs={{0,4},{4,8},{8,12},{12,16},{16,20},{20,24},{24,28},{1,5},{5,9},{9,... | collective-permute-start | bytes 122888 | tf_op jit(solution)/shard_map/ppermute | solution.py:18
  155.2 0.0 collective-permute-done.3
  155.2 1.6 collective-permute-done.4
  156.8 1.3 collective-permute-start.5
  158.1 3.0 collective-permute-start.6
  161.2 0.0 collective-permute-done.5
  161.2 0.8 collective-permute-done.6
  162.0 0.3 select_maximum_fusion.8
  162.3 0.9 multiply_reduce_fusion.3
  163.3 43.2 %all-reduce.5 = (f32[]{:T(128)}, f32[]{:T(128)}) all-reduce(f32[]{:T(128)} %get-tuple-element.105, f32[]{:T(128)} %get-tuple-element.104), channel_id=1, replica_groups=mesh['band'=8,'space'=4] {'band','space'}, use_global_device_ids=true, to_apply=%region_3.4 | all-reduce | flops 2 | bytes 16 | tf_op jit(solution)/shard_map/psum | solution.py:41
  207.7 1.3 collective-permute-start.7
  209.0 4.8 %collective-permute-start.8 = (f32[2,40,128]{2,1,0:T(8,128)S(1)}, f32[2,40,128]{2,1,0:T(8,128)S(1)}, u32[]{:S(2)}, u32[]{:S(2)}) collective-permute-start(f32[2,40,128]{2,1,0:T(8,128)S(1)} %get-tuple-element.138), channel_id=1, source_target_pairs={{0,4},{4,8},{8,12},{12,16},{16,20},{20,24},{24,28},{1,5},{5,9},{9,... | collective-permute-start | bytes 122888 | tf_op jit(solution)/shard_map/ppermute | solution.py:18
  213.8 0.0 collective-permute-done.7
  213.9 1.6 collective-permute-done.8
  215.5 1.3 collective-permute-start.10
  216.8 1.3 collective-permute-start.9
  218.1 0.0 collective-permute-done.10
  218.1 4.2 %collective-permute-done.9 = f32[12,2,128]{2,1,0:T(2,128)S(1)} collective-permute-done((f32[12,2,128]{2,1,0:T(2,128)S(1)}, f32[12,2,128]{2,1,0:T(2,128)S(1)}, u32[]{:S(2)}, u32[]{:S(2)}) %collective-permute-start.9) | collective-permute-done | bytes 12320 | tf_op jit(solution)/shard_map/ppermute | solution.py:19
  222.4 0.3 select_maximum_fusion.4
  222.6 0.9 multiply_reduce_fusion.1
  223.6 43.0 %all-reduce.4 = (f32[]{:T(128)}, f32[]{:T(128)}) all-reduce(f32[]{:T(128)} %get-tuple-element.103, f32[]{:T(128)} %get-tuple-element.102), channel_id=1, replica_groups=mesh['band'=8,'space'=4] {'band','space'}, use_global_device_ids=true, to_apply=%region_7.8 | all-reduce | flops 2 | bytes 16 | tf_op jit(solution)/shard_map/psum | solution.py:41
  271.1 1.3 collective-permute-start.11
  272.4 4.8 %collective-permute-start.12 = (f32[2,40,128]{2,1,0:T(8,128)S(1)}, f32[2,40,128]{2,1,0:T(8,128)S(1)}, u32[]{:S(2)}, u32[]{:S(2)}) collective-permute-start(f32[2,40,128]{2,1,0:T(8,128)S(1)} %get-tuple-element.136), channel_id=1, source_target_pairs={{0,4},{4,8},{8,12},{12,16},{16,20},{20,24},{24,28},{1,5},{5,9},{9,... | collective-permute-start | bytes 122888 | tf_op jit(solution)/shard_map/ppermute | solution.py:18
  277.2 0.0 collective-permute-done.11
  277.2 1.6 collective-permute-done.12
  278.8 1.3 collective-permute-start.13
  280.1 3.0 collective-permute-start.14
  283.2 0.0 collective-permute-done.13
  283.2 0.8 collective-permute-done.14
  284.0 0.3 select_maximum_fusion
  284.3 0.9 fusion.39
  285.2 44.6 %all-reduce.3 = (f32[]{:T(128)}, f32[]{:T(128)}) all-reduce(f32[]{:T(128)} %get-tuple-element.101, f32[]{:T(128)} %get-tuple-element.100), channel_id=1, replica_groups=mesh['band'=8,'space'=4] {'band','space'}, use_global_device_ids=true, to_apply=%region_11.12 | all-reduce | flops 2 | bytes 16 | tf_op jit(solution)/shard_map/psum | solution.py:41
  333.6 0.7 multiply_add_fusion
  (13 shorter events, 0.3 us)
Async XLA Ops:
  29.0 31.8 %collective-permute-start = (f32[64,40,128]{2,1,0:T(8,128)S(1)}, f32[64,40,128]{2,1,0:T(8,128)S(1)}, u32[]{:S(2)}, u32[]{:S(2)}) collective-permute-start(f32[64,40,128]{2,1,0:T(8,128)S(1)} %get-tuple-element.84), channel_id=1, source_target_pairs={{0,4},{4,0},{8,12},{12,8},{16,20},{20,16},{24,28},{28,24},{1,5},{5... | collective-permute-start | bytes 3932168 | tf_op jit(solution)/shard_map/ppermute | solution.py:55
  61.0 30.0 %collective-permute-start.1 = (f32[64,40,128]{2,1,0:T(8,128)S(1)}, f32[64,40,128]{2,1,0:T(8,128)S(1)}, u32[]{:S(2)}, u32[]{:S(2)}) collective-permute-start(f32[64,40,128]{2,1,0:T(8,128)S(1)} %add.174), channel_id=1, source_target_pairs={{0,8},{4,12},{8,0},{12,4},{16,24},{20,28},{24,16},{28,20},{1,9},{5... | collective-permute-start | bytes 3932168 | tf_op jit(solution)/shard_map/ppermute | solution.py:55
  91.1 58.1 %collective-permute-start.2 = (f32[64,40,128]{2,1,0:T(8,128)S(1)}, f32[64,40,128]{2,1,0:T(8,128)S(1)}, u32[]{:S(2)}, u32[]{:S(2)}) collective-permute-start(f32[64,40,128]{2,1,0:T(8,128)S(1)} %add.175), channel_id=1, source_target_pairs={{0,16},{4,20},{8,24},{12,28},{16,0},{20,4},{24,8},{28,12},{1,17},{... | collective-permute-start | bytes 3932168 | tf_op jit(solution)/shard_map/ppermute | solution.py:55
  149.3 5.9 %collective-permute-start.3 = (f32[2,40,128]{2,1,0:T(8,128)S(1)}, f32[2,40,128]{2,1,0:T(8,128)S(1)}, u32[]{:S(2)}, u32[]{:S(2)}) collective-permute-start(f32[2,40,128]{2,1,0:T(8,128)S(1)} %get-tuple-element.141), channel_id=1, source_target_pairs={{4,0},{8,4},{12,8},{16,12},{20,16},{24,20},{28,24},{5,1},{9,5},{13... | collective-permute-start | bytes 122888 | tf_op jit(solution)/shard_map/ppermute | solution.py:19
  150.6 6.2 %collective-permute-start.4 = (f32[2,40,128]{2,1,0:T(8,128)S(1)}, f32[2,40,128]{2,1,0:T(8,128)S(1)}, u32[]{:S(2)}, u32[]{:S(2)}) collective-permute-start(f32[2,40,128]{2,1,0:T(8,128)S(1)} %get-tuple-element.140), channel_id=1, source_target_pairs={{0,4},{4,8},{8,12},{12,16},{16,20},{20,24},{24,28},{1,5},{5,9},{9,... | collective-permute-start | bytes 122888 | tf_op jit(solution)/shard_map/ppermute | solution.py:18
  156.8 4.3 %collective-permute-start.5 = (f32[12,2,128]{2,1,0:T(2,128)S(1)}, f32[12,2,128]{2,1,0:T(2,128)S(1)}, u32[]{:S(2)}, u32[]{:S(2)}) collective-permute-start(f32[12,2,128]{2,1,0:T(2,128)S(1)} %get-tuple-element.135), channel_id=1, source_target_pairs={{1,0},{2,1},{3,2},{5,4},{6,5},{7,6},{9,8},{10,9},{11,10},{13,12},{... | collective-permute-start | bytes 36872 | tf_op jit(solution)/shard_map/ppermute | solution.py:19
  158.1 3.9 %collective-permute-start.6 = (f32[12,2,128]{2,1,0:T(2,128)S(1)}, f32[12,2,128]{2,1,0:T(2,128)S(1)}, u32[]{:S(2)}, u32[]{:S(2)}) collective-permute-start(f32[12,2,128]{2,1,0:T(2,128)S(1)} %get-tuple-element.134), channel_id=1, source_target_pairs={{0,1},{1,2},{2,3},{4,5},{5,6},{6,7},{8,9},{9,10},{10,11},{12,13},{... | collective-permute-start | bytes 36872 | tf_op jit(solution)/shard_map/ppermute | solution.py:18
  207.7 6.2 %collective-permute-start.7 = (f32[2,40,128]{2,1,0:T(8,128)S(1)}, f32[2,40,128]{2,1,0:T(8,128)S(1)}, u32[]{:S(2)}, u32[]{:S(2)}) collective-permute-start(f32[2,40,128]{2,1,0:T(8,128)S(1)} %get-tuple-element.139), channel_id=1, source_target_pairs={{4,0},{8,4},{12,8},{16,12},{20,16},{24,20},{28,24},{5,1},{9,5},{13... | collective-permute-start | bytes 122888 | tf_op jit(solution)/shard_map/ppermute | solution.py:19
  209.0 6.5 %collective-permute-start.8 = (f32[2,40,128]{2,1,0:T(8,128)S(1)}, f32[2,40,128]{2,1,0:T(8,128)S(1)}, u32[]{:S(2)}, u32[]{:S(2)}) collective-permute-start(f32[2,40,128]{2,1,0:T(8,128)S(1)} %get-tuple-element.138), channel_id=1, source_target_pairs={{0,4},{4,8},{8,12},{12,16},{16,20},{20,24},{24,28},{1,5},{5,9},{9,... | collective-permute-start | bytes 122888 | tf_op jit(solution)/shard_map/ppermute | solution.py:18
  215.5 2.6 collective-permute-start.10
  216.8 5.5 %collective-permute-start.9 = (f32[12,2,128]{2,1,0:T(2,128)S(1)}, f32[12,2,128]{2,1,0:T(2,128)S(1)}, u32[]{:S(2)}, u32[]{:S(2)}) collective-permute-start(f32[12,2,128]{2,1,0:T(2,128)S(1)} %get-tuple-element.131), channel_id=1, source_target_pairs={{1,0},{2,1},{3,2},{5,4},{6,5},{7,6},{9,8},{10,9},{11,10},{13,12},{... | collective-permute-start | bytes 36872 | tf_op jit(solution)/shard_map/ppermute | solution.py:19
  271.1 6.2 %collective-permute-start.11 = (f32[2,40,128]{2,1,0:T(8,128)S(1)}, f32[2,40,128]{2,1,0:T(8,128)S(1)}, u32[]{:S(2)}, u32[]{:S(2)}) collective-permute-start(f32[2,40,128]{2,1,0:T(8,128)S(1)} %get-tuple-element.137), channel_id=1, source_target_pairs={{4,0},{8,4},{12,8},{16,12},{20,16},{24,20},{28,24},{5,1},{9,5},{13... | collective-permute-start | bytes 122888 | tf_op jit(solution)/shard_map/ppermute | solution.py:19
  272.4 6.5 %collective-permute-start.12 = (f32[2,40,128]{2,1,0:T(8,128)S(1)}, f32[2,40,128]{2,1,0:T(8,128)S(1)}, u32[]{:S(2)}, u32[]{:S(2)}) collective-permute-start(f32[2,40,128]{2,1,0:T(8,128)S(1)} %get-tuple-element.136), channel_id=1, source_target_pairs={{0,4},{4,8},{8,12},{12,16},{16,20},{20,24},{24,28},{1,5},{5,9},{9,... | collective-permute-start | bytes 122888 | tf_op jit(solution)/shard_map/ppermute | solution.py:18
  278.8 4.3 %collective-permute-start.13 = (f32[12,2,128]{2,1,0:T(2,128)S(1)}, f32[12,2,128]{2,1,0:T(2,128)S(1)}, u32[]{:S(2)}, u32[]{:S(2)}) collective-permute-start(f32[12,2,128]{2,1,0:T(2,128)S(1)} %get-tuple-element.127), channel_id=1, source_target_pairs={{1,0},{2,1},{3,2},{5,4},{6,5},{7,6},{9,8},{10,9},{11,10},{13,12},{... | collective-permute-start | bytes 36872 | tf_op jit(solution)/shard_map/ppermute | solution.py:19
  280.1 3.9 %collective-permute-start.14 = (f32[12,2,128]{2,1,0:T(2,128)S(1)}, f32[12,2,128]{2,1,0:T(2,128)S(1)}, u32[]{:S(2)}, u32[]{:S(2)}) collective-permute-start(f32[12,2,128]{2,1,0:T(2,128)S(1)} %get-tuple-element.126), channel_id=1, source_target_pairs={{0,1},{1,2},{2,3},{4,5},{5,6},{6,7},{8,9},{9,10},{10,11},{12,13},{... | collective-permute-start | bytes 36872 | tf_op jit(solution)/shard_map/ppermute | solution.py:18
